TPU v7x, 32 devices: a whole 2x2x4 slice. The times are simulated.
32 devices in a mesh: dp: 8 (over z, x), mp: 4 (over y, core).
Axes of the slice: x: 2, y: 2, z: 4, core: 2. Of those that a mesh axis runs over, the one named last changes fastest.
Arguments:
- tokens: bfloat16 [16384, 1024], P('dp'), may hold values from -6 to 6
- segment_ids: int32 [8, 2048], P('dp'), may hold values from 0 to 127, never falling along the last dimension, each value on 1 to 512 neighbouring positions
- w_query: bfloat16 [1024, 1024], P(None, 'mp'), may hold values from -0.1875 to 0.1875
- w_key: bfloat16 [1024, 1024], P(None, 'mp'), may hold values from -0.1875 to 0.1875
- w_value: bfloat16 [1024, 1024], P(None, 'mp'), may hold values from -0.1875 to 0.1875
- w_gate: bfloat16 [1024, 1024], P(None, 'mp'), may hold values from -0.1875 to 0.1875
- w_out: bfloat16 [1024, 1024], P('mp'), may hold values from -0.25 to 0.25
- w_left: bfloat16 [1024, 2816], P(None, 'mp'), may hold values from -0.1875 to 0.1875
- w_right: bfloat16 [1024, 2816], P(None, 'mp'), may hold values from -0.1875 to 0.1875
- w_down: bfloat16 [2816, 1024], P('mp'), may hold values from -0.109375 to 0.109375
- cotangent: bfloat16 [16384, 1024], P('dp'), may hold values from -6 to 6
Outputs:
- output: bfloat16 [16384, 1024], P('dp')
- grad_tokens: bfloat16 [16384, 1024], P('dp')
- grad_w_query: float32 [1024, 1024], P('dp', 'mp')
- grad_w_key: float32 [1024, 1024], P('dp', 'mp')
- grad_w_value: float32 [1024, 1024], P('dp', 'mp')
- grad_w_gate: float32 [1024, 1024], P('dp', 'mp')
- grad_w_out: float32 [1024, 1024], P('mp', 'dp')
- grad_w_left: float32 [1024, 2816], P('dp', 'mp')
- grad_w_right: float32 [1024, 2816], P('dp', 'mp')
- grad_w_down: float32 [2816, 1024], P('mp', 'dp')
Inputs may be any that keep to these rules, and one draw needn't show every extreme that they name: `segment_ids`: in each row of 2048 positions the ids never fall; a document spans 1 to 512 positions, and one of them exactly that many.
All inputs are finite; a program needn't handle non-finite values.
Results may differ from a plain program's by a relative error of at most 0.02.
Values may be sent and summed in bfloat16 or wider, within the bound.
A program may use at most 192 MiB of HBM per device.

v0:
```python
import jax
import jax.numpy as jnp
from jax import lax
from jax.sharding import PartitionSpec as P

HD = 64
BLOCK = 64


def head_total(partial_value):
    return lax.psum(partial_value.astype(jnp.bfloat16), "mp").astype(jnp.float32)


def scatter_sum(grads):
    joined = jnp.concatenate([g.astype(jnp.bfloat16) for g in grads], axis=1)
    summed = lax.psum_scatter(joined, "dp", scatter_dimension=0, tiled=True).astype(jnp.float32)
    cuts = []
    at = 0
    for g in grads:
        cuts.append(summed[:, at : at + g.shape[1]])
        at += g.shape[1]
    return cuts


def rms_factor(values):
    return lax.rsqrt(jnp.mean(values * values, axis=-1, keepdims=True) + 1e-06)


def norm_back(grad, normed, factor):
    return factor * (grad - normed * jnp.mean(grad * normed, axis=-1, keepdims=True))


def block_scores(query_blocks, key_blocks, allowed):
    scores = jnp.einsum(
        "bqhd,bkhd->bhqk", query_blocks, key_blocks, preferred_element_type=jnp.float32
    ) * HD ** (-0.5)
    return jnp.where(allowed[:, None], scores, jnp.float32(-1e30))


def body(
    tokens, segment_ids, w_query, w_key, w_value, w_gate, w_out, w_left, w_right, w_down, cotangent
):
    rows_all = tokens.shape[0]
    width_c = w_query.shape[1]
    heads_here = width_c // HD
    blocks = rows_all // BLOCK
    source = tokens.astype(jnp.float32)
    recip_one = rms_factor(source)
    normed_one = source * recip_one
    normed_low = normed_one.astype(jnp.bfloat16)
    queries = jnp.dot(normed_low, w_query, preferred_element_type=jnp.float32).astype(jnp.bfloat16)
    keys_all = jnp.dot(normed_low, w_key, preferred_element_type=jnp.float32).astype(jnp.bfloat16)
    values_all = jnp.dot(normed_low, w_value, preferred_element_type=jnp.float32).astype(
        jnp.bfloat16
    )
    gate_pre = jnp.dot(normed_low, w_gate, preferred_element_type=jnp.float32).reshape(
        rows_all, heads_here, HD
    )
    query_blocks = queries.reshape(blocks, BLOCK, heads_here, HD)
    key_blocks = keys_all.reshape(blocks, BLOCK, heads_here, HD)
    value_blocks = values_all.reshape(blocks, BLOCK, heads_here, HD)
    seg_blocks = segment_ids.reshape(blocks, BLOCK)
    lower = jnp.arange(BLOCK)[:, None] >= jnp.arange(BLOCK)[None, :]
    allowed = (seg_blocks[:, :, None] == seg_blocks[:, None, :]) & lower[None]
    masked = block_scores(query_blocks, key_blocks, allowed)
    top = jnp.max(masked, axis=-1, keepdims=True)
    expd = jnp.exp(masked - top)
    total = jnp.sum(expd, axis=-1, keepdims=True)
    log_total = top + jnp.log(total)
    probs_low = (expd / total).astype(jnp.bfloat16)
    attended = jnp.einsum(
        "bhqk,bkhd->bqhd", probs_low, value_blocks, preferred_element_type=jnp.float32
    )
    attended = attended.reshape(rows_all, heads_here, HD)
    head_factor = rms_factor(attended)
    head_normed = attended * head_factor
    sigma = jax.nn.sigmoid(gate_pre)
    gated = (head_normed * sigma).reshape(rows_all, width_c).astype(jnp.bfloat16)
    attn_sum = head_total(jnp.dot(gated, w_out, preferred_element_type=jnp.float32))
    hidden = source + attn_sum
    recip_two = rms_factor(hidden)
    normed_two = hidden * recip_two
    normed_two_low = normed_two.astype(jnp.bfloat16)
    left = jnp.dot(normed_two_low, w_left, preferred_element_type=jnp.float32)
    right = jnp.dot(normed_two_low, w_right, preferred_element_type=jnp.float32)
    mixed = (left * right).astype(jnp.bfloat16)
    glu_sum = head_total(jnp.dot(mixed, w_down, preferred_element_type=jnp.float32))
    output = (hidden + glu_sum).astype(jnp.bfloat16)
    grad_down = jnp.einsum("tc,tf->cf", cotangent, mixed, preferred_element_type=jnp.float32)
    d_mixed = jnp.einsum("tc,fc->tf", cotangent, w_down, preferred_element_type=jnp.float32)
    d_left = (d_mixed * right).astype(jnp.bfloat16)
    d_right = (d_mixed * left).astype(jnp.bfloat16)
    grad_left = jnp.einsum("td,tf->df", normed_two_low, d_left, preferred_element_type=jnp.float32)
    grad_right = jnp.einsum(
        "td,tf->df", normed_two_low, d_right, preferred_element_type=jnp.float32
    )
    glu_grads = scatter_sum((grad_left, grad_right, grad_down))
    d_partial_two = jnp.einsum("tf,df->td", d_left, w_left, preferred_element_type=jnp.float32)
    d_partial_two = d_partial_two + jnp.einsum(
        "tf,df->td", d_right, w_right, preferred_element_type=jnp.float32
    )
    d_norm_two = head_total(d_partial_two)
    d_hidden = cotangent.astype(jnp.float32) + norm_back(d_norm_two, normed_two, recip_two)
    d_out_low = d_hidden.astype(jnp.bfloat16)
    grad_out = jnp.einsum("td,tc->dc", d_out_low, gated, preferred_element_type=jnp.float32)
    d_gated = jnp.einsum("td,cd->tc", d_out_low, w_out, preferred_element_type=jnp.float32)
    d_gated = d_gated.reshape(rows_all, heads_here, HD)
    d_head = d_gated * sigma
    d_gate = (
        (d_gated * head_normed * sigma * (1.0 - sigma))
        .reshape(rows_all, width_c)
        .astype(jnp.bfloat16)
    )
    d_attended = norm_back(d_head, head_normed, head_factor).astype(jnp.bfloat16)
    d_attended = d_attended.reshape(blocks, BLOCK, heads_here, HD)
    probs = jnp.exp(block_scores(query_blocks, key_blocks, allowed) - log_total)
    probs_back = probs.astype(jnp.bfloat16)
    d_probs = jnp.einsum(
        "bqhd,bkhd->bhqk", d_attended, value_blocks, preferred_element_type=jnp.float32
    )
    d_values = jnp.einsum(
        "bhqk,bqhd->bkhd", probs_back, d_attended, preferred_element_type=jnp.float32
    )
    delta_rows = jnp.sum(probs * d_probs, axis=-1, keepdims=True)
    d_scores = (probs * (d_probs - delta_rows)).astype(jnp.bfloat16)
    d_queries = jnp.einsum(
        "bhqk,bkhd->bqhd", d_scores, key_blocks, preferred_element_type=jnp.float32
    ) * HD ** (-0.5)
    d_keys = jnp.einsum(
        "bhqk,bqhd->bkhd", d_scores, query_blocks, preferred_element_type=jnp.float32
    ) * HD ** (-0.5)
    d_queries = d_queries.reshape(rows_all, width_c).astype(jnp.bfloat16)
    d_keys = d_keys.reshape(rows_all, width_c).astype(jnp.bfloat16)
    d_values = d_values.reshape(rows_all, width_c).astype(jnp.bfloat16)
    grad_query = jnp.einsum("td,tc->dc", normed_low, d_queries, preferred_element_type=jnp.float32)
    grad_key = jnp.einsum("td,tc->dc", normed_low, d_keys, preferred_element_type=jnp.float32)
    grad_value = jnp.einsum("td,tc->dc", normed_low, d_values, preferred_element_type=jnp.float32)
    grad_gate = jnp.einsum("td,tc->dc", normed_low, d_gate, preferred_element_type=jnp.float32)
    attn_grads = scatter_sum((grad_query, grad_key, grad_value, grad_gate, grad_out))
    d_partial_one = jnp.einsum("tc,dc->td", d_queries, w_query, preferred_element_type=jnp.float32)
    d_partial_one = d_partial_one + jnp.einsum(
        "tc,dc->td", d_keys, w_key, preferred_element_type=jnp.float32
    )
    d_partial_one = d_partial_one + jnp.einsum(
        "tc,dc->td", d_values, w_value, preferred_element_type=jnp.float32
    )
    d_partial_one = d_partial_one + jnp.einsum(
        "tc,dc->td", d_gate, w_gate, preferred_element_type=jnp.float32
    )
    d_norm_one = head_total(d_partial_one)
    d_source = d_hidden + norm_back(d_norm_one, normed_one, recip_one)
    grad_tokens = d_source.astype(jnp.bfloat16)
    return (
        output,
        grad_tokens,
        attn_grads[0],
        attn_grads[1],
        attn_grads[2],
        attn_grads[3],
        attn_grads[4].T,
        glu_grads[0],
        glu_grads[1],
        glu_grads[2].T,
    )


def solution(mesh):
    in_specs = (
        P("dp", None),
        P("dp", None),
        P(None, "mp"),
        P(None, "mp"),
        P(None, "mp"),
        P(None, "mp"),
        P("mp", None),
        P(None, "mp"),
        P(None, "mp"),
        P("mp", None),
        P("dp", None),
    )
    out_specs = (
        P("dp", None),
        P("dp", None),
        P("dp", "mp"),
        P("dp", "mp"),
        P("dp", "mp"),
        P("dp", "mp"),
        P("mp", "dp"),
        P("dp", "mp"),
        P("dp", "mp"),
        P("mp", "dp"),
    )
    return jax.shard_map(body, mesh=mesh, in_specs=in_specs, out_specs=out_specs, check_vma=False)
```

profile of v0, /device:TPU:0, one launch (start us, length us, event | category | flops | bytes accessed | tf_op | source)
XLA Modules:
  0.0 696.8 jit_solution(10704735771133625387)
XLA Ops:
  22.1 5.3 convolution_convert_fusion.3
  27.4 4.4 reshape.149
  36.0 4.5 convolution_convert_fusion.4
  40.5 4.9 reshape.148
  57.3 6.6 copy.67
  67.6 5.4 multiply_convert_fusion.7
  77.3 88.3 %all-reduce.5.cloned.1.call-done = bf16[2048,1024]{1,0:T(8,128)(2,1)} async-done(((bf16[2048,1024]{1,0:T(8,128)(2,1)}), bf16[2048,1024]{1,0:T(8,128)(2,1)}) %all-reduce.5.cloned.1.call-update) | async-done | bytes 4194320 | tf_op jit(solution)/shard_map/psum | solution.py:11
  165.6 5.0 multiply_reduce_fusion
  179.5 5.5 multiply_convert_fusion
  185.0 6.0 fusion.51
  191.1 5.5 add_convert_fusion.1
  196.7 5.0 reshape.154
  203.2 6.9 convolution_convert_fusion
  210.1 72.3 %all-reduce.7.cloned.1.call-done = bf16[2048,1024]{1,0:T(8,128)(2,1)} async-done(((bf16[2048,1024]{1,0:T(8,128)(2,1)}), bf16[2048,1024]{1,0:T(8,128)(2,1)}) %all-reduce.7.cloned.1.call-update) | async-done | bytes 4194320 | tf_op jit(solution)/shard_map/psum | solution.py:11
  282.4 6.6 fusion.3
  290.7 5.0 fusion.5
  300.5 5.2 reshape.155
  305.8 6.6 fusion.14
  326.7 5.6 copy.77
  332.3 4.2 convert_element_type.166
  346.2 4.7 fusion.53
  350.9 4.6 fusion.52
  355.5 9.9 %add_convert_fusion = bf16[2048,1024]{1,0:T(8,128)(2,1)} fusion(f32[2048,1024]{1,0:T(8,128)S(1)} %fusion.54, f32[2048,1024]{1,0:T(8,128)} %fusion.52, f32[2048,1024]{1,0:T(8,128)} %fusion.53, bf16[2048,256]{0,1:T(8,128)(2,1)S(1)} %copy-done.36, bf16[1024,256]{1,0:T(8,128)(2,1)S(1)} %copy-done.38), kind=kOutput, calls=%fused_computation.17 | convolution fusion | flops 1082130432 | bytes 30932992 | tf_op jit(solution)/shard_map/tc,dc->td/dot_general | solution.py:147
  365.4 4.4 fusion.45
  378.2 4.5 copy.95
  383.0 6.4 convolution_convert_fusion.5
  398.2 6.6 copy.97
  404.8 113.8 %all-reduce.9.cloned.1.call-done = (bf16[2048,1024]{1,0:T(8,128)(2,1)}, bf16[2048,1024]{1,0:T(8,128)(2,1)}) async-done(((bf16[2048,1024]{1,0:T(8,128)(2,1)}, bf16[2048,1024]{1,0:T(8,128)(2,1)}), (bf16[2048,1024]{1,0:T(8,128)(2,1)}, bf16[2048,1024]{1,0:T(8,128)(2,1)})) %all-reduce.9.cloned.1.call-update) | async-done | bytes 8388624 | tf_op jit(solution)/shard_map/psum | solution.py:11
  518.6 4.5 fusion.9
  524.5 9.8 %fusion.8 = (bf16[2048,1024]{1,0:T(8,128)(2,1)}, bf16[2048,1024]{1,0:T(8,128)(2,1)}) fusion(f32[2048,1024]{1,0:T(8,128)} %copy-done.6, bf16[2048,1024]{1,0:T(8,128)(2,1)} %get-tuple-element.41, bf16[2048,1024]{1,0:T(8,128)(2,1)S(1)} %copy-done.5, f32[2048]{0:T(1024)S(1)} %broadcast_multiply_fusion.1, f32[2048]{0:T(1024)S(1)} %copy-done.51, ...), kind=kLoop, calls=%fused_computation.14 | loop fusion | flops 27262976 | bytes 33570816 | tf_op jit(solution)/shard_map/convert_element_type | solution.py:152
  534.3 58.6 %reduce-scatter.7.cloned.1.call-done = bf16[128,1280]{1,0:T(8,128)(2,1)} async-done(((bf16[1024,1280]{1,0:T(8,128)(2,1)}), bf16[128,1280]{1,0:T(8,128)(2,1)}) %reduce-scatter.7.cloned.1.call-update) | async-done | bytes 327696
  597.9 89.7 %reduce-scatter.9.cloned.1.call-done = bf16[128,2112]{1,0:T(8,128)(2,1)} async-done(((bf16[1024,2112]{1,0:T(8,128)(2,1)}), bf16[128,2112]{1,0:T(8,128)(2,1)}) %reduce-scatter.9.cloned.1.call-update) | async-done | bytes 540688
  (185 shorter events, 106.0 us)
Async XLA Ops:
  7.2 172.3 %copy-start = (bf16[704,1024]{1,0:T(8,128)(2,1)S(1)}, bf16[704,1024]{1,0:T(8,128)(2,1)}, u32[]{:S(2)}) copy-start(bf16[704,1024]{1,0:T(8,128)(2,1)} %param.20) | copy-start | bytes 4325380
  7.2 158.4 %all-reduce.5.cloned.1.call-start = ((), (), s32[]{:S(2)}) async-start(), calls=%async_computation.2 | async-start | bytes 8388608 | tf_op jit(solution)/shard_map/psum | solution.py:11
  22.1 24.3 %copy-start.17 = (bf16[32,64,4,64]{1,3,2,0:T(8,128)(2,1)}, bf16[32,64,4,64]{1,3,2,0:T(8,128)(2,1)S(1)}, u32[]{:S(2)}) copy-start(bf16[32,64,4,64]{1,3,2,0:T(8,128)(2,1)S(1)} %copy.74) | copy-start | bytes 3145732
  49.2 6.7 copy-start.7
  49.3 6.7 copy-start.42
  67.6 6.3 copy-start.39
  77.2 205.1 %all-reduce.7.cloned.1.call-start = ((), (), s32[]{:S(2)}) async-start(), calls=%async_computation.3 | async-start | bytes 8388608 | tf_op jit(solution)/shard_map/psum | solution.py:11
  165.6 5.0 copy-start.3
  165.6 5.9 copy-start.9
  185.0 6.0 copy-start.25
  185.0 6.0 copy-start.27
  185.0 6.0 copy-start.54
  196.6 321.9 %all-reduce.9.cloned.1.call-start = ((), (), s32[]{:S(2)}) async-start(), calls=%async_computation.6 | async-start | bytes 16777216 | tf_op jit(solution)/shard_map/psum | solution.py:11
  282.4 6.7 copy-start.4
  282.4 7.1 %copy-start.10 = (bf16[2048,1024]{1,0:T(8,128)(2,1)S(1)}, bf16[2048,1024]{1,0:T(8,128)(2,1)}, u32[]{:S(2)}) copy-start(bf16[2048,1024]{1,0:T(8,128)(2,1)} %all-reduce.5.cloned.1.call-done) | copy-start | bytes 12582916
  282.4 8.3 %copy-start.13 = (bf16[2048,1024]{1,0:T(8,128)(2,1)S(1)}, bf16[2048,1024]{1,0:T(8,128)(2,1)}, u32[]{:S(2)}) copy-start(bf16[2048,1024]{1,0:T(8,128)(2,1)} %param.21) | copy-start | bytes 12582916
  290.7 5.1 copy-start.15
  290.7 5.1 copy-start.29
  290.7 5.1 copy-start.40
  290.7 5.1 copy-start.45
  300.3 5.4 copy-start.44
  305.7 6.6 copy-start.8
  305.8 6.6 copy-start.41
  326.7 9.8 %copy-start.32 = (bf16[32,64,4,64]{3,1,2,0:T(8,128)(2,1)S(1)}, bf16[32,64,4,64]{3,1,2,0:T(8,128)(2,1)}, u32[]{:S(2)}) copy-start(bf16[32,64,4,64]{3,1,2,0:T(8,128)(2,1)} %fusion.34) | copy-start | bytes 3145732
  365.4 227.5 %reduce-scatter.7.cloned.1.call-start = ((), (), s32[]{:S(2)}) async-start(), calls=%async_computation.4 | async-start | bytes 2949120
  369.8 6.3 slice-start
  382.7 304.9 %reduce-scatter.9.cloned.1.call-start = ((), (), s32[]{:S(2)}) async-start(), calls=%async_computation.5 | async-start | bytes 5013504
  382.9 6.4 copy-start.26
  383.0 6.4 copy-start.35
  404.7 113.8 %copy-start.51 = (f32[2048]{0:T(1024)S(1)}, f32[2048]{0:T(1024)}, u32[]{:S(2)}) copy-start(f32[2048]{0:T(1024)} %copy-done.50) | copy-start | bytes 24580
  518.6 5.9 copy-start.11
  592.9 97.2 %copy-start.1 = (bf16[704,1024]{1,0:T(8,128)(2,1)S(1)}, bf16[704,1024]{1,0:T(8,128)(2,1)}, u32[]{:S(2)}) copy-start(bf16[704,1024]{1,0:T(8,128)(2,1)} %param.20) | copy-start | bytes 4325380
  (30 other events, 88.8 us)
Sparse Core Ops, SparseCore 0:
  77.4 88.1 all-reduce.4
  196.7 85.6 all-reduce.6
  365.5 153.0 all-reduce.8
  521.9 70.8 reduce-scatter.6
  596.3 91.2 reduce-scatter.8
where the time goes:
time: 705 us; the launch traced here: 697 us
  waiting for transfers between devices  423 us (60%)
  matrix products  115 us (16%)
  local copies, waits for them, and re-layouts  89.2 us (13%)
  other arithmetic  54.5 us (8%)
  between operations  14.7 us (2%)
    psum x3, waiting for transfers between devices, head_total(): lax.psum(partial_value.astype(jnp.bfloat16), 'mp').astype(jnp.float32)  274 us
    unnamed x7, waiting for transfers between devices  148 us
    unnamed x123, local copies, waits for them, and re-layouts  27.9 us
  transfers between devices with their start and end apart: 5, of which 5 were waited for; matrix products, arithmetic and copies ran while one was open for 10% of the time, Pallas kernels for 0%

commit v1 on v0

--- a/solution.py
+++ b/solution.py
@@ -8,7 +8,9 @@
 
 
 def head_total(partial_value):
-    return lax.psum(partial_value.astype(jnp.bfloat16), "mp").astype(jnp.float32)
+    return jnp.sum(lax.all_gather(partial_value.astype(jnp.bfloat16), "mp"), axis=0).astype(
+        jnp.float32
+    )
 
 
 def scatter_sum(grads):

time: 705 us -> 754 us (1.070)
  other arithmetic: 54.5 us -> 101 us
  matrix products: 115 us -> 123 us
    all_gather x0 -> x4, waiting for transfers between devices: none -> 372 us  [head_total(): lax.all_gather(partial_value.astype(jnp.bfloat16), 'mp')]
    psum x3 -> x0, waiting for transfers between devices: 274 us -> none  [head_total(): lax.psum(partial_value.astype(jnp.bfloat16), 'mp').astype(jnp.float32)]
    unnamed x7 -> x8, waiting for transfers between devices: 148 us -> 46.6 us
    reduce_sum x0 -> x4, other arithmetic: none -> 49.4 us  [head_total(): jnp.sum(lax.all_gather(partial_value.astype(jnp.bfloat16), 'mp'), axis=0)]
  transfers between devices with their start and end apart: 5 -> 6, of which waited for: 5 -> 5; matrix products, arithmetic and copies ran while one was open for 10% -> 24% of each run, Pallas kernels for 0% -> 0%
where the time goes in v1:
time: 754 us; the launch traced here: 746 us
  waiting for transfers between devices  418 us (55%)
  matrix products  123 us (16%)
  other arithmetic  101 us (13%)
  local copies, waits for them, and re-layouts  88.3 us (12%)
  between operations  15 us (2%)
    all_gather x4, waiting for transfers between devices, head_total(): lax.all_gather(partial_value.astype(jnp.bfloat16), 'mp')  372 us
    reduce_sum x4, other arithmetic, head_total(): jnp.sum(lax.all_gather(partial_value.astype(jnp.bfloat16), 'mp'), axis=0)  49.4 us
    unnamed x8, waiting for transfers between devices  46.6 us
    unnamed x123, local copies, waits for them, and re-layouts  29.1 us
  transfers between devices with their start and end apart: 6, of which 5 were waited for; matrix products, arithmetic and copies ran while one was open for 24% of the time, Pallas kernels for 0%

profile of v1, /device:TPU:0, one launch (start us, length us, event | category | flops | bytes accessed | tf_op | source)
XLA Modules:
  0.0 746.2 jit_solution(3804545798659255427)
XLA Ops:
  32.3 5.3 convolution_convert_fusion.4
  37.6 4.6 reshape.148
  54.2 6.6 copy.67
  64.4 6.0 multiply_convert_fusion.7
  74.8 108.7 %all-gather.9.cloned.1.call-done = bf16[8192,1024]{1,0:T(8,128)(2,1)} async-done(((bf16[2048,1024]{1,0:T(8,128)(2,1)}), bf16[8192,1024]{1,0:T(8,128)(2,1)}) %all-gather.9.cloned.1.call-update) | async-done | bytes 16777232 | tf_op jit(solution)/shard_map/all_gather | solution.py:11
  183.6 12.3 %reduce_sum.123 = bf16[2048,1024]{1,0:T(8,128)(2,1)} reduce(bf16[4,2048,1024]{2,1,0:T(8,128)(2,1)} %bitcast.116, bf16[]{:T(256)} %constant.28.clone.1), dimensions={0}, to_apply=%region_4.5 | reduce | flops 6291456 | bytes 20971522 | tf_op jit(solution)/shard_map/reduce_sum | solution.py:11
  195.9 5.0 multiply_reduce_fusion
  209.6 5.5 multiply_convert_fusion
  216.7 5.0 convolution_convert_fusion
  222.2 5.5 fusion.51
  227.8 5.3 add_convert_fusion.1
  233.2 7.5 %convolution_convert_fusion.5 = bf16[1024,704]{0,1:T(8,128)(2,1)S(1)} fusion(bf16[2048,704]{0,1:T(8,128)(2,1)} %get-tuple-element.44, bf16[2048,1024]{1,0:T(8,128)(2,1)} %copy-done.34), kind=kOutput, calls=%fused_computation.66 | convolution fusion | flops 2953510912 | bytes 8519680 | tf_op jit(solution)/shard_map/td,tf->df/dot_general | solution.py:96
  250.1 6.4 copy.97
  256.7 5.0 reshape.154
  261.8 66.0 %all-gather.11.cloned.1.call-done = bf16[8192,1024]{1,0:T(8,128)(2,1)} async-done(((bf16[2048,1024]{1,0:T(8,128)(2,1)}), bf16[8192,1024]{1,0:T(8,128)(2,1)}) %all-gather.11.cloned.1.call-update) | async-done | bytes 16777232 | tf_op jit(solution)/shard_map/all_gather | solution.py:11
  327.8 12.8 %reduce_sum.125 = bf16[2048,1024]{1,0:T(8,128)(2,1)} reduce(bf16[4,2048,1024]{2,1,0:T(8,128)(2,1)} %bitcast.113, bf16[]{:T(256)} %constant.28.clone.1), dimensions={0}, to_apply=%region_6.7 | reduce | flops 6291456 | bytes 20971522 | tf_op jit(solution)/shard_map/reduce_sum | solution.py:11
  340.6 94.7 %all-gather.13.cloned.1.call-done = bf16[8192,1024]{1,0:T(8,128)(2,1)} async-done(((bf16[2048,1024]{1,0:T(8,128)(2,1)}), bf16[8192,1024]{1,0:T(8,128)(2,1)}) %all-gather.13.cloned.1.call-update) | async-done | bytes 16777232 | tf_op jit(solution)/shard_map/all_gather | solution.py:11
  435.3 12.1 %reduce_sum.126 = bf16[2048,1024]{1,0:T(8,128)(2,1)} reduce(bf16[4,2048,1024]{2,1,0:T(8,128)(2,1)} %bitcast.115, bf16[]{:T(256)} %constant.28.clone.1), dimensions={0}, to_apply=%region_7.8 | reduce | flops 6291456 | bytes 20971522 | tf_op jit(solution)/shard_map/reduce_sum | solution.py:11
  447.4 6.8 fusion.3
  455.8 7.2 fusion.5
  463.1 7.0 multiply_reduce_fusion.3
  475.2 6.6 fusion.14
  489.3 4.7 multiply_reduce_fusion.1
  498.2 5.3 copy.77
  503.5 4.6 convert_element_type.174
  519.4 4.8 fusion.45
  544.4 4.7 fusion.52
  549.1 10.0 %add_convert_fusion = bf16[2048,1024]{1,0:T(8,128)(2,1)} fusion(f32[2048,1024]{1,0:T(8,128)S(1)} %fusion.54, f32[2048,1024]{1,0:T(8,128)} %fusion.52, f32[2048,1024]{1,0:T(8,128)} %fusion.53, bf16[2048,256]{0,1:T(8,128)(2,1)S(1)} %copy-done.36, bf16[1024,256]{1,0:T(8,128)(2,1)S(1)} %copy-done.37), kind=kOutput, calls=%fused_computation.17 | convolution fusion | flops 1082130432 | bytes 30932992 | tf_op jit(solution)/shard_map/tc,dc->td/dot_general | solution.py:149
  561.6 46.5 %reduce-scatter.7.cloned.1.call-done = bf16[128,1280]{1,0:T(8,128)(2,1)} async-done(((bf16[1024,1280]{1,0:T(8,128)(2,1)}), bf16[128,1280]{1,0:T(8,128)(2,1)}) %reduce-scatter.7.cloned.1.call-update) | async-done | bytes 327696
  613.0 102.1 %all-gather.15.cloned.1.call-done = bf16[8192,1024]{1,0:T(8,128)(2,1)} async-done(((bf16[2048,1024]{1,0:T(8,128)(2,1)}), bf16[8192,1024]{1,0:T(8,128)(2,1)}) %all-gather.15.cloned.1.call-update) | async-done | bytes 16777232 | tf_op jit(solution)/shard_map/all_gather | solution.py:11
  715.1 12.1 %reduce_sum.130 = bf16[2048,1024]{1,0:T(8,128)(2,1)} reduce(bf16[4,2048,1024]{2,1,0:T(8,128)(2,1)} %bitcast.114, bf16[]{:T(256)} %constant.28.clone.1), dimensions={0}, to_apply=%region_11.12 | reduce | flops 6291456 | bytes 20971522 | tf_op jit(solution)/shard_map/reduce_sum | solution.py:11
  733.2 6.0 fusion.8
  (192 shorter events, 128.3 us)
Async XLA Ops:
  7.2 202.4 %copy-start = (bf16[704,1024]{1,0:T(8,128)(2,1)S(1)}, bf16[704,1024]{1,0:T(8,128)(2,1)}, u32[]{:S(2)}) copy-start(bf16[704,1024]{1,0:T(8,128)(2,1)} %param.20) | copy-start | bytes 4325380
  7.2 176.4 %all-gather.9.cloned.1.call-start = ((), (), s32[]{:S(2)}) async-start(), calls=%async_computation.2 | async-start | bytes 20971520 | tf_op jit(solution)/shard_map/all_gather | solution.py:11
  32.3 11.0 %copy-start.19 = (bf16[32,64,4,64]{1,3,2,0:T(8,128)(2,1)}, bf16[32,64,4,64]{1,3,2,0:T(8,128)(2,1)S(1)}, u32[]{:S(2)}) copy-start(bf16[32,64,4,64]{1,3,2,0:T(8,128)(2,1)S(1)} %copy.78) | copy-start | bytes 3145732
  46.1 6.6 copy-start.7
  46.1 6.6 copy-start.40
  64.4 6.1 copy-start.16
  64.4 7.0 copy-start.38
  74.8 253.0 %all-gather.11.cloned.1.call-start = ((), (), s32[]{:S(2)}) async-start(), calls=%async_computation.3 | async-start | bytes 20971520 | tf_op jit(solution)/shard_map/all_gather | solution.py:11
  195.9 5.9 copy-start.10
  221.7 213.6 %all-gather.13.cloned.1.call-start = ((), (), s32[]{:S(2)}) async-start(), calls=%async_computation.4 | async-start | bytes 20971520 | tf_op jit(solution)/shard_map/all_gather | solution.py:11
  222.2 5.6 copy-start.28
  222.2 5.6 copy-start.54
  233.1 326.0 %reduce-scatter.9.cloned.1.call-start = ((), (), s32[]{:S(2)}) async-start(), calls=%async_computation.7 | async-start | bytes 5013504
  233.2 7.5 %copy-start.27 = (bf16[2048,704]{0,1:T(8,128)(2,1)S(1)}, bf16[2048,704]{0,1:T(8,128)(2,1)}, u32[]{:S(2)}) copy-start(bf16[2048,704]{0,1:T(8,128)(2,1)} %get-tuple-element.46) | copy-start | bytes 8650756
  233.2 8.1 %copy-start.35 = (bf16[2048,1024]{1,0:T(8,128)(2,1)S(1)}, bf16[2048,1024]{1,0:T(8,128)(2,1)}, u32[]{:S(2)}) copy-start(bf16[2048,1024]{1,0:T(8,128)(2,1)} %copy-done.34) | copy-start | bytes 12582916
  256.5 5.3 copy-start.41
  256.5 351.5 %reduce-scatter.7.cloned.1.call-start = ((), (), s32[]{:S(2)}) async-start(), calls=%async_computation.6 | async-start | bytes 2949120
  447.4 6.8 copy-start.4
  447.4 7.2 copy-start.11
  447.4 8.4 %copy-start.13 = (bf16[2048,1024]{1,0:T(8,128)(2,1)S(1)}, bf16[2048,1024]{1,0:T(8,128)(2,1)}, u32[]{:S(2)}) copy-start(bf16[2048,1024]{1,0:T(8,128)(2,1)} %reduce_sum.126) | copy-start | bytes 12582916
  455.8 7.2 copy-start.39
  455.8 7.2 copy-start.44
  463.0 7.0 copy-start.6
  463.1 7.0 copy-start.17
  463.1 7.0 copy-start.18
  475.2 6.7 copy-start.8
  489.3 37.0 %copy-start.30 = (bf16[2048,256]{0,1:T(8,128)(2,1)}, bf16[2048,256]{0,1:T(8,128)(2,1)S(1)}, u32[]{:S(2)}) copy-start(bf16[2048,256]{0,1:T(8,128)(2,1)S(1)} %convert_element_type.181) | copy-start | bytes 3145732
  524.2 6.3 slice-start
  537.1 178.0 %all-gather.15.cloned.1.call-start = ((), (), s32[]{:S(2)}) async-start(), calls=%async_computation.5 | async-start | bytes 20971520 | tf_op jit(solution)/shard_map/all_gather | solution.py:11
  715.1 12.1 %copy-start.51 = (f32[2048]{0:T(1024)S(1)}, f32[2048]{0:T(1024)}, u32[]{:S(2)}) copy-start(f32[2048]{0:T(1024)} %copy-done.50) | copy-start | bytes 24580
  727.3 5.9 copy-start.12
  733.2 6.0 copy-start.1
  (31 other events, 99.9 us)
Sparse Core Ops, SparseCore 0:
  74.9 108.6 all-gather.8
  221.9 105.8 all-gather.10
  329.4 105.8 all-gather.12
  438.8 92.0 reduce-scatter.8
  537.2 70.7 reduce-scatter.6
  610.0 105.0 all-gather.14
